TPU v7x, 32 devices: a whole 2x2x4 slice. The times are simulated.
32 devices in a mesh: segment: 4 (over y, core), dp: 8 (over z, x).
Axes of the slice: x: 2, y: 2, z: 4, core: 2. Of those that a mesh axis runs over, the one named last changes fastest.
Arguments:
- token_ids: int32 [1024], P('dp'), may hold values from 0 to 38015, as said below
- table: bfloat16 [4752, 28672], P('segment', 'dp'), may hold values from -6 to 6
- out_grad: bfloat16 [1024, 3584], P('dp', 'segment'), may hold values from -6 to 6
Outputs:
- embedded: bfloat16 [1024, 3584], P('dp')
- table_grad: bfloat16 [4752, 28672], P('segment', 'dp')
Inputs may be any that keep to these rules, and one draw needn't show every extreme that they name: `token_ids`: in the 128 tokens of each data group, at most 16 ids lie in one segment's slice of 9504 rows with one residue modulo 8; in every data group some segment and residue has exactly 16.
All inputs are finite; a program needn't handle non-finite values.
Results may differ from a plain program's by a relative error of at most 0.001.
Values may be sent and summed in bfloat16 or wider, within the bound.
A program may use at most 64 MiB of HBM per device.

v0:
```python
import jax
import jax.numpy as jnp
from jax import lax
from jax.sharding import PartitionSpec as P

D = 3584
PACK = 8


def body(token_ids, table, out_grad):
    lines = table.shape[0]
    width = table.shape[1]
    groups = lax.axis_size("dp")
    tok_rows = token_ids.shape[0]
    quarters = D // width
    slot = lax.axis_index("dp") // quarters
    first = lax.axis_index("segment") * lines * PACK
    every_id = lax.all_gather(token_ids, "dp", axis=0, tiled=True)
    local = every_id - first
    in_section = (local >= 0) & (local < lines * PACK)
    owned = in_section & (local % PACK == slot)
    line_idx = jnp.clip(local // PACK, 0, lines - 1)
    whole_grad = lax.all_gather(out_grad, "segment", axis=1, tiled=True)
    capacity = tok_rows // PACK
    owned_grid = owned.reshape(groups, tok_rows)
    rank = jnp.cumsum(owned_grid.astype(jnp.int32), axis=1) - 1
    place = jnp.where(owned_grid, rank, capacity)
    group_rows = jnp.broadcast_to(jnp.arange(groups, dtype=jnp.int32)[:, None], (groups, tok_rows))
    row_of = (
        jnp.zeros((groups, capacity), jnp.int32)
        .at[group_rows, place]
        .set(line_idx.reshape(groups, tok_rows), mode="drop")
    )
    filled = jnp.zeros((groups, capacity), jnp.bool_).at[group_rows, place].set(True, mode="drop")
    fetched = jnp.take(table, row_of.reshape(-1), axis=0).reshape(groups, capacity, width)
    fetched = jnp.where(filled[:, :, None], fetched, jnp.zeros((), jnp.bfloat16))
    arrived = lax.all_to_all(fetched, "dp", split_axis=0, concat_axis=0, tiled=True)
    my_local = token_ids - first
    my_in = (my_local >= 0) & (my_local < lines * PACK)
    my_slot = my_local % PACK
    slot_hits = (my_slot[:, None] == jnp.arange(PACK, dtype=jnp.int32)[None, :]) & my_in[:, None]
    slot_ranks = jnp.cumsum(slot_hits.astype(jnp.int32), axis=0) - 1
    my_rank = jnp.sum(jnp.where(slot_hits, slot_ranks, 0), axis=1)
    sources = my_slot[:, None] * quarters + jnp.arange(quarters, dtype=jnp.int32)[None, :]
    flat_index = jnp.clip(sources * capacity + my_rank[:, None], 0, groups * capacity - 1)
    gathered = jnp.take(
        arrived.reshape(groups * capacity, width), flat_index.reshape(-1), axis=0
    ).reshape(tok_rows, D)
    segment_part = jnp.where(my_in[:, None], gathered.astype(jnp.float32), 0.0)
    slot_place = jnp.where(my_in, my_slot, PACK)
    token_at = (
        jnp.zeros((PACK, capacity), jnp.int32)
        .at[slot_place, my_rank]
        .set(jnp.arange(tok_rows, dtype=jnp.int32), mode="drop")
    )
    valid = jnp.zeros((PACK, capacity), jnp.bool_).at[slot_place, my_rank].set(True, mode="drop")
    grad_pick = jnp.take(whole_grad, token_at.reshape(-1), axis=0).reshape(
        PACK, capacity, quarters, width
    )
    grad_pick = jnp.where(valid[:, :, None, None], grad_pick, jnp.zeros((), jnp.bfloat16))
    grad_send = grad_pick.transpose(0, 2, 1, 3).reshape(groups, capacity, width)
    returned = lax.all_to_all(grad_send, "dp", split_axis=0, concat_axis=0, tiled=True)
    target = jnp.where(filled, row_of, lines)
    accum = (
        jnp.zeros((lines, width), jnp.float32)
        .at[target.reshape(-1)]
        .add(returned.reshape(-1, width).astype(jnp.float32), mode="drop")
    )
    embedded = lax.psum(segment_part.astype(jnp.bfloat16), "segment")
    return (embedded, accum.astype(jnp.bfloat16))


def solution(mesh):
    placed = (P("dp"), P("segment", "dp"), P("dp", "segment"))
    return jax.shard_map(
        body,
        mesh=mesh,
        in_specs=placed,
        out_specs=(P("dp", None), P("segment", "dp")),
        check_vma=False,
    )
```

profile of v0, /device:TPU:0, one launch (start us, length us, event | category | flops | bytes accessed | tf_op | source)
XLA Modules:
  0.0 159.1 jit_solution(7434590179938538914)
XLA Ops:
  7.2 0.0 copy-start.1
  7.2 0.0 copy-start
  7.2 22.6 %all-gather = s32[8,1,128]{2,1,0:T(1,128)S(1)} all-gather(s32[1,1,128]{2,1,0:T(1,128)} %bitcast.39), channel_id=1, replica_groups=mesh['segment'=4,'dp'=8] {'dp'}, dimensions={0}, use_global_device_ids=true | all-gather | bytes 4608 | tf_op jit(solution)/shard_map/all_gather | solution.py:18
  29.8 0.3 copy.12
  30.1 0.3 copy.13
  30.4 23.6 %compare_select_fusion = s32[8,128,1]{2,0,1:T(8,128)S(1)} fusion(pred[8,128,1]{2,0,1:T(8,128)(4,1)S(1)} %copy.13, s32[8,128,1]{2,0,1:T(8,128)S(1)} %copy.12), kind=kOutput, calls=%fused_computation.12 | output fusion | flops 135168 | bytes 9216 | tf_op jit(solution)/shard_map/jit(cumsum)/reduce_window_sum | solution.py:26
  54.0 0.2 copy.14
  54.2 0.8 multiply_reduce_fusion
  55.0 0.1 copy.19
  55.1 0.7 and_reduce_fusion
  55.8 0.1 copy.18
  56.0 4.3 %scatter_custom_fusion.4 = s32[128]{0:T(128)S(1)} fusion(s32[1024]{0:T(1024)S(1)} %bitcast.40, s32[1024]{0:T(1024)S(1)} %fusion.6, s32[]{:T(128)} %constant.70.clone.1), kind=kCustom, calls=%fused_computation.66 | custom fusion | bytes 516
  60.3 0.1 reshape.189
  60.4 4.3 %scatter_custom_fusion.3 = pred[128]{0:T(512)(128)(4,1)S(1)} fusion(s32[1024]{0:T(1024)S(1)} %bitcast.41, pred[1024]{0:T(1024)(128)(4,1)S(1)} %broadcast.224, pred[]{:T(512)} %constant.71.clone.1), kind=kCustom, calls=%fused_computation.56 | custom fusion | bytes 129
  64.8 0.1 reshape.185
  64.9 6.6 %gather_fusion = bf16[128,3584]{1,0:T(8,128)(2,1)S(1)} fusion(bf16[1188,3584]{1,0:T(8,128)(2,1)} %param.6, s32[1024]{0:T(1024)S(1)} %pad_clamp_fusion.2), kind=kCustom, calls=%fused_computation.2 | custom fusion | bytes 1835520 | tf_op jit(solution)/shard_map/jit(_take)/gather | solution.py:35
  71.4 1.1 select_select_fusion
  72.6 3.6 %all-to-all-start = ((bf16[8,16,3584]{2,1,0:T(8,128)(2,1)}), bf16[8,16,3584]{2,1,0:T(8,128)(2,1)S(1)}, u32[]{:S(2)}, u32[]{:S(2)}) async-start(bf16[8,16,3584]{2,1,0:T(8,128)(2,1)} %select_select_fusion), calls=%async_computation | async-start | bytes 1835008 | tf_op jit(solution)/shard_map/all_to_all | solution.py:37
  76.1 0.0 copy-done.1
  76.2 0.1 fusion.4
  76.3 0.2 reduce_window_sum.23
  76.4 0.2 select_reduce_fusion
  76.7 6.4 %scatter_fusion.1 = s32[8,16]{1,0:T(8,128)S(1)} fusion(s32[8,16]{1,0:T(8,128)S(1)} %broadcast.169, s32[128]{0:T(128)S(1)} %fusion.18, s32[128]{0:T(128)S(1)} %iota.14), kind=kCustom, calls=%fused_computation.4 | custom fusion | bytes 2560 | tf_op jit(solution)/shard_map/scatter | solution.py:54
  83.0 0.1 reshape.180
  83.1 0.0 copy-done
  83.2 9.5 %all_gather.7 = bf16[128,3584]{1,0:T(8,128)(2,1)S(1)} all-gather(bf16[128,896]{1,0:T(8,128)(2,1)S(1)} %copy-done), channel_id=1, replica_groups=mesh['segment'=4,'dp'=8] {'segment'}, dimensions={1}, use_global_device_ids=true | all-gather | bytes 1146880 | tf_op jit(solution)/shard_map/all_gather | solution.py:23
  92.7 1.1 gather_fusion.2
  93.8 6.5 %scatter_fusion = pred[8,16]{1,0:T(8,128)(4,1)S(1)} fusion(pred[8,16]{1,0:T(8,128)(4,1)S(1)} %broadcast.166, s32[128]{0:T(128)S(1)} %fusion.18, pred[128]{0:T(512)(128)(4,1)S(1)} %broadcast.225), kind=kCustom, calls=%fused_computation.3 | custom fusion | bytes 1408 | tf_op jit(solution)/shard_map/scatter | solution.py:56
  100.3 0.2 broadcast_select_fusion
  100.5 1.1 broadcast_select_fusion.1
  101.5 0.0 all-to-all-done
  101.5 5.9 %all-to-all-start.1 = ((bf16[8,16,3584]{2,1,0:T(8,128)(2,1)}), bf16[8,16,3584]{2,1,0:T(8,128)(2,1)S(1)}, u32[]{:S(2)}, u32[]{:S(2)}) async-start(bf16[8,16,3584]{2,1,0:T(8,128)(2,1)} %broadcast_select_fusion.1), calls=%async_computation.1 | async-start | bytes 1835008 | tf_op jit(solution)/shard_map/all_to_all | solution.py:62
  107.5 0.0 all-reduce.2.cloned.1.call-start
  107.5 1.1 gather_fusion.1
  108.7 1.3 select_convert_fusion
  109.9 0.0 all-reduce.2.cloned.1.call-update
  110.0 0.1 reshape.179
  110.1 20.9 %all-to-all-done.1 = bf16[8,16,3584]{2,1,0:T(8,128)(2,1)S(1)} async-done(((bf16[8,16,3584]{2,1,0:T(8,128)(2,1)}), bf16[8,16,3584]{2,1,0:T(8,128)(2,1)S(1)}, u32[]{:S(2)}, u32[]{:S(2)}) %all-to-all-start.1) | async-done | bytes 917536 | tf_op jit(solution)/shard_map/all_to_all | solution.py:62
  130.9 10.0 %scatter_custom_fusion.2 = f32[1188,3584]{1,0:T(8,128)} fusion(s32[128]{0:T(128)S(1)} %fusion.16, f32[]{:T(128)} %constant.121.clone.1, bf16[128,3584]{1,0:T(8,128)(2,1)S(1)} %bitcast.35), kind=kCustom, calls=%fused_computation.8 | custom fusion | flops 917504 | bytes 17948676 | tf_op jit(solution)/shard_map/scatter-add | solution.py:67
  140.9 9.1 %convert_element_type.32 = bf16[1188,3584]{1,0:T(8,128)(2,1)} convert(f32[1188,3584]{1,0:T(8,128)} %scatter_custom_fusion.2) | non-fusion elementwise | flops 4257792 | bytes 25546752 | tf_op jit(solution)/shard_map/convert_element_type | solution.py:70
  150.1 0.0 all-reduce.2.cloned.1.call-done
  150.1 2.2 %copy.23 = bf16[128,3584]{1,0:T(8,128)(2,1)} copy(bf16[128,3584]{1,0:T(8,128)(2,1)} %all-reduce.2.cloned.1.call-done) | data formatting | bytes 1835008
  (24 shorter events, 0.2 us)
Async XLA Ops:
  7.2 69.0 %copy-start.1 = (s32[128]{0:T(128)S(1)}, s32[128]{0:T(128)}, u32[]{:S(2)}) copy-start(s32[128]{0:T(128)} %param.5) | copy-start | bytes 1540
  7.2 76.0 %copy-start = (bf16[128,896]{1,0:T(8,128)(2,1)S(1)}, bf16[128,896]{1,0:T(8,128)(2,1)}, u32[]{:S(2)}) copy-start(bf16[128,896]{1,0:T(8,128)(2,1)} %param.7) | copy-start | bytes 688132
  72.6 29.0 %all-to-all-start = ((bf16[8,16,3584]{2,1,0:T(8,128)(2,1)}), bf16[8,16,3584]{2,1,0:T(8,128)(2,1)S(1)}, u32[]{:S(2)}, u32[]{:S(2)}) async-start(bf16[8,16,3584]{2,1,0:T(8,128)(2,1)} %select_select_fusion), calls=%async_computation | async-start | bytes 1835008 | tf_op jit(solution)/shard_map/all_to_all | solution.py:37
  101.5 29.4 %all-to-all-start.1 = ((bf16[8,16,3584]{2,1,0:T(8,128)(2,1)}), bf16[8,16,3584]{2,1,0:T(8,128)(2,1)S(1)}, u32[]{:S(2)}, u32[]{:S(2)}) async-start(bf16[8,16,3584]{2,1,0:T(8,128)(2,1)} %broadcast_select_fusion.1), calls=%async_computation.1 | async-start | bytes 1835008 | tf_op jit(solution)/shard_map/all_to_all | solution.py:62
  107.5 42.6 %all-reduce.2.cloned.1.call-start = ((), (), s32[]{:S(2)}) async-start(), calls=%async_computation.2 | async-start | bytes 1835008 | tf_op jit(solution)/shard_map/psum | solution.py:69
Sparse Core Ops, SparseCore 0:
  111.2 36.2 all-reduce.1
where the time goes:
time: 159 us
  other arithmetic  48.5 us (31%)
  local copies, waits for them, and re-layouts  33.8 us (21%)
  blocking collectives  32.1 us (20%)
  waiting for transfers between devices  20.9 us (13%)
  between operations  14.3 us (9%)
  starting transfers between devices  9.52 us (6%)
    another operation x1, other arithmetic, body(): rank = jnp.cumsum(owned_grid.astype(jnp.int32), axis=1) - 1  23.6 us
    all_gather x1, blocking collectives, body(): every_id = lax.all_gather(token_ids, 'dp', axis=0, tiled=True)  22.6 us
    all_to_all x1, waiting for transfers between devices, body(): lax.all_to_all(grad_send, 'dp', split_axis=0, concat_axis=0, tiled=True)  20.9 us
    unnamed x11, local copies, waits for them, and re-layouts  11.1 us
    scatter-add x1, other arithmetic, body(): accum = jnp.zeros((lines, width), jnp.float32).at[target.reshape(-1)].add...  10 us
    all_gather x1, blocking collectives, body(): whole_grad = lax.all_gather(out_grad, 'segment', axis=1, tiled=True)  9.52 us
    convert_element_type x1, other arithmetic, body(): return (embedded, accum.astype(jnp.bfloat16))  9.14 us
    gather x1, local copies, waits for them, and re-layouts, body(): jnp.take(table, row_of.reshape(-1), axis=0).reshape(groups, capacity, width)  6.55 us
  transfers between devices with their start and end apart: 3, of which 1 were waited for; matrix products, arithmetic and copies ran while one was open for 24% of the time, Pallas kernels for 0%

commit v1 on v0

--- a/solution.py
+++ b/solution.py
@@ -15,7 +15,9 @@
     quarters = D // width
     slot = lax.axis_index("dp") // quarters
     first = lax.axis_index("segment") * lines * PACK
-    every_id = lax.all_gather(token_ids, "dp", axis=0, tiled=True)
+    every_id = jnp.concatenate(
+        lax.all_to_all(jnp.stack([token_ids] * lax.axis_size("dp")), "dp", 0, 0), axis=0
+    )
     local = every_id - first
     in_section = (local >= 0) & (local < lines * PACK)
     owned = in_section & (local % PACK == slot)

time: 159 us -> 145 us (0.912)
  other arithmetic: 48.5 us -> 25.9 us
  blocking collectives: 32.1 us -> 9.55 us
  waiting for transfers between devices: 20.9 us -> 42.8 us
  starting transfers between devices: 9.52 us -> 17 us
    another operation x1, other arithmetic: 23.6 us -> 0.45 us  [body(): rank = jnp.cumsum(owned_grid.astype(jnp.int32), axis=1) - 1]
    all_gather x1 -> x0, blocking collectives: 22.6 us -> none  [body(): every_id = lax.all_gather(token_ids, 'dp', axis=0, tiled=True)]
    all_to_all x1, waiting for transfers between devices: 0.01 us -> 22.2 us  [body(): lax.all_to_all(fetched, 'dp', split_axis=0, concat_axis=0, tiled=True)]
    all_to_all x0 -> x1, starting transfers between devices: none -> 7.28 us  [body(): lax.all_to_all(jnp.stack([token_ids] * lax.axis_size('dp')), 'dp', 0, 0)]
    all_to_all x1, starting transfers between devices: 3.55 us -> 6 us  [body(): lax.all_to_all(fetched, 'dp', split_axis=0, concat_axis=0, tiled=True)]
    all_to_all x1, starting transfers between devices: 5.93 us -> 3.64 us  [body(): lax.all_to_all(grad_send, 'dp', split_axis=0, concat_axis=0, tiled=True)]
    unnamed x11 -> x10, local copies, waits for them, and re-layouts: 11.1 us -> 11 us
  transfers between devices with their start and end apart: 3 -> 4, of which waited for: 1 -> 2; matrix products, arithmetic and copies ran while one was open for 24% -> 27% of each run, Pallas kernels for 0% -> 0%
where the time goes in v1:
time: 145 us
  waiting for transfers between devices  42.8 us (30%)
  local copies, waits for them, and re-layouts  35.2 us (24%)
  other arithmetic  25.9 us (18%)
  starting transfers between devices  17 us (12%)
  between operations  14.3 us (10%)
  blocking collectives  9.55 us (7%)
    all_to_all x1, waiting for transfers between devices, body(): lax.all_to_all(fetched, 'dp', split_axis=0, concat_axis=0, tiled=True)  22.2 us
    all_to_all x1, waiting for transfers between devices, body(): lax.all_to_all(grad_send, 'dp', split_axis=0, concat_axis=0, tiled=True)  20.5 us
    unnamed x10, local copies, waits for them, and re-layouts  11 us
    scatter-add x1, other arithmetic, body(): accum = jnp.zeros((lines, width), jnp.float32).at[target.reshape(-1)].add...  10 us
    all_gather x1, blocking collectives, body(): whole_grad = lax.all_gather(out_grad, 'segment', axis=1, tiled=True)  9.55 us
    convert_element_type x1, other arithmetic, body(): return (embedded, accum.astype(jnp.bfloat16))  9.13 us
    all_to_all x1, starting transfers between devices, body(): lax.all_to_all(jnp.stack([token_ids] * lax.axis_size('dp')), 'dp', 0, 0)  7.28 us
    gather x1, local copies, waits for them, and re-layouts, body(): jnp.take(table, row_of.reshape(-1), axis=0).reshape(groups, capacity, width)  6.56 us
  transfers between devices with their start and end apart: 4, of which 2 were waited for; matrix products, arithmetic and copies ran while one was open for 27% of the time, Pallas kernels for 0%

profile of v1, /device:TPU:0, one launch (start us, length us, event | category | flops | bytes accessed | tf_op | source)
XLA Modules:
  0.0 144.7 jit_solution(2342754970033430063)
XLA Ops:
  7.2 0.0 copy-start.2
  7.2 0.0 copy-start.1
  7.2 1.3 stack.2
  8.4 7.3 %all-to-all-start = ((s32[8,1,128]{2,1,0:T(1,128)}), s32[8,1,128]{2,1,0:T(1,128)S(1)}, u32[]{:S(2)}, u32[]{:S(2)}) async-start(s32[8,1,128]{2,1,0:T(1,128)} %stack.2), calls=%async_computation | async-start | bytes 8192 | tf_op jit(solution)/shard_map/all_to_all | solution.py:19
  15.7 0.7 compare_and_fusion.3
  16.4 0.7 and_select_fusion
  17.1 0.1 fusion.23
  17.2 0.2 reduce_window_sum.23
  17.3 0.2 select_reduce_fusion
  17.5 0.7 fusion.36
  18.2 6.4 %scatter_fusion.1 = s32[8,16]{1,0:T(8,128)S(1)} fusion(s32[8,16]{1,0:T(8,128)S(1)} %broadcast.283, s32[128]{0:T(128)S(1)} %fusion.36, s32[128]{0:T(128)S(1)} %iota.14), kind=kCustom, calls=%fused_computation.4 | custom fusion | bytes 2560 | tf_op jit(solution)/shard_map/scatter | solution.py:56
  24.6 0.1 reshape.235
  24.7 9.6 %all_gather.3 = bf16[128,3584]{1,0:T(8,128)(2,1)S(1)} all-gather(bf16[128,896]{1,0:T(8,128)(2,1)} %param.7), channel_id=1, replica_groups=mesh['segment'=4,'dp'=8] {'segment'}, dimensions={1}, use_global_device_ids=true | all-gather | bytes 1146880 | tf_op jit(solution)/shard_map/all_gather | solution.py:25
  34.2 1.1 gather_fusion.2
  35.4 6.5 %scatter_fusion = pred[8,16]{1,0:T(8,128)(4,1)S(1)} fusion(pred[8,16]{1,0:T(8,128)(4,1)S(1)} %broadcast.281, s32[128]{0:T(128)S(1)} %fusion.36, pred[128]{0:T(512)(128)(4,1)S(1)} %broadcast.339), kind=kCustom, calls=%fused_computation.3 | custom fusion | bytes 1408 | tf_op jit(solution)/shard_map/scatter | solution.py:58
  41.9 0.0 all-to-all-done
  41.9 0.3 copy.25
  42.2 0.5 broadcast_compare_fusion
  42.7 0.2 copy.32
  42.9 0.2 copy.31
  43.1 0.2 copy.30
  43.4 0.0 copy-done.2
  43.4 0.1 multiply_reduce_fusion
  43.4 0.0 copy-done.1
  43.4 0.1 and_reduce_fusion
  43.5 4.3 %scatter_custom_fusion.4 = s32[128]{0:T(128)S(1)} fusion(s32[1024]{0:T(1024)S(1)} %get-tuple-element.8, s32[1024]{0:T(1024)S(1)} %get-tuple-element.7, s32[]{:T(128)} %constant.108.clone.1), kind=kCustom, calls=%fused_computation.86 | custom fusion | bytes 516
  47.9 0.1 reshape.244
  47.9 4.5 %scatter_custom_fusion.3 = pred[128]{0:T(512)(128)(4,1)S(1)} fusion(s32[1024]{0:T(1024)S(1)} %get-tuple-element.8, pred[1024]{0:T(1024)(128)(4,1)S(1)} %broadcast.338, pred[]{:T(512)} %constant.109.clone.1), kind=kCustom, calls=%fused_computation.76 | custom fusion | bytes 129
  52.5 0.1 reshape.240
  52.6 0.0 copy-start
  52.6 6.6 %gather_fusion = bf16[128,3584]{1,0:T(8,128)(2,1)S(1)} fusion(bf16[1188,3584]{1,0:T(8,128)(2,1)} %param.6, s32[1024]{0:T(1024)S(1)} %pad_clamp_fusion.2), kind=kCustom, calls=%fused_computation.2 | custom fusion | bytes 1835520 | tf_op jit(solution)/shard_map/jit(_take)/gather | solution.py:37
  59.2 1.1 select_select_fusion
  60.3 6.0 %all-to-all-start.1 = ((bf16[8,16,3584]{2,1,0:T(8,128)(2,1)}), bf16[8,16,3584]{2,1,0:T(8,128)(2,1)S(1)}, u32[]{:S(2)}, u32[]{:S(2)}) async-start(bf16[8,16,3584]{2,1,0:T(8,128)(2,1)} %select_select_fusion), calls=%async_computation.1 | async-start | bytes 1835008 | tf_op jit(solution)/shard_map/all_to_all | solution.py:39
  66.3 0.1 broadcast_select_fusion
  66.4 1.1 broadcast_select_fusion.1
  67.5 22.2 %all-to-all-done.1 = bf16[8,16,3584]{2,1,0:T(8,128)(2,1)S(1)} async-done(((bf16[8,16,3584]{2,1,0:T(8,128)(2,1)}), bf16[8,16,3584]{2,1,0:T(8,128)(2,1)S(1)}, u32[]{:S(2)}, u32[]{:S(2)}) %all-to-all-start.1) | async-done | bytes 917536 | tf_op jit(solution)/shard_map/all_to_all | solution.py:39
  89.8 3.6 %all-to-all-start.2 = ((bf16[8,16,3584]{2,1,0:T(8,128)(2,1)}), bf16[8,16,3584]{2,1,0:T(8,128)(2,1)S(1)}, u32[]{:S(2)}, u32[]{:S(2)}) async-start(bf16[8,16,3584]{2,1,0:T(8,128)(2,1)} %broadcast_select_fusion.1), calls=%async_computation.2 | async-start | bytes 1835008 | tf_op jit(solution)/shard_map/all_to_all | solution.py:64
  93.4 0.0 all-reduce.2.cloned.1.call-start
  93.4 0.0 copy-done
  93.5 1.1 gather_fusion.1
  94.6 1.3 select_convert_fusion
  95.9 0.0 all-reduce.2.cloned.1.call-update
  95.9 0.1 reshape.234
  96.0 20.5 %all-to-all-done.2 = bf16[8,16,3584]{2,1,0:T(8,128)(2,1)S(1)} async-done(((bf16[8,16,3584]{2,1,0:T(8,128)(2,1)}), bf16[8,16,3584]{2,1,0:T(8,128)(2,1)S(1)}, u32[]{:S(2)}, u32[]{:S(2)}) %all-to-all-start.2) | async-done | bytes 917536 | tf_op jit(solution)/shard_map/all_to_all | solution.py:64
  116.5 10.0 %scatter_custom_fusion.2 = f32[1188,3584]{1,0:T(8,128)} fusion(s32[128]{0:T(128)S(1)} %fusion.34, f32[]{:T(128)} %constant.123.clone.1, bf16[128,3584]{1,0:T(8,128)(2,1)S(1)} %bitcast.49), kind=kCustom, calls=%fused_computation.8 | custom fusion | flops 917504 | bytes 17948676 | tf_op jit(solution)/shard_map/scatter-add | solution.py:69
  126.6 9.1 %convert_element_type.32 = bf16[1188,3584]{1,0:T(8,128)(2,1)} convert(f32[1188,3584]{1,0:T(8,128)} %scatter_custom_fusion.2) | non-fusion elementwise | flops 4257792 | bytes 25546752 | tf_op jit(solution)/shard_map/convert_element_type | solution.py:72
  135.7 0.0 all-reduce.2.cloned.1.call-done
  135.7 2.2 %copy.42 = bf16[128,3584]{1,0:T(8,128)(2,1)} copy(bf16[128,3584]{1,0:T(8,128)(2,1)} %all-reduce.2.cloned.1.call-done) | data formatting | bytes 1835008
  (20 shorter events, 0.2 us)
Async XLA Ops:
  7.2 36.2 %copy-start.2 = (s32[2]{0:T(128)S(1)}, s32[2]{0:T(128)}, u32[]{:S(2)}) copy-start(s32[2]{0:T(128)} %constant.124) | copy-start | bytes 28
  7.2 36.3 %copy-start.1 = (s32[2]{0:T(128)S(1)}, s32[2]{0:T(128)}, u32[]{:S(2)}) copy-start(s32[2]{0:T(128)} %constant.127) | copy-start | bytes 28
  8.4 33.4 %all-to-all-start = ((s32[8,1,128]{2,1,0:T(1,128)}), s32[8,1,128]{2,1,0:T(1,128)S(1)}, u32[]{:S(2)}, u32[]{:S(2)}) async-start(s32[8,1,128]{2,1,0:T(1,128)} %stack.2), calls=%async_computation | async-start | bytes 8192 | tf_op jit(solution)/shard_map/all_to_all | solution.py:19
  52.6 40.9 %copy-start = (s32[128]{0:T(128)S(1)}, s32[128]{0:T(128)}, u32[]{:S(2)}) copy-start(s32[128]{0:T(128)} %param.5) | copy-start | bytes 1540
  60.3 29.5 %all-to-all-start.1 = ((bf16[8,16,3584]{2,1,0:T(8,128)(2,1)}), bf16[8,16,3584]{2,1,0:T(8,128)(2,1)S(1)}, u32[]{:S(2)}, u32[]{:S(2)}) async-start(bf16[8,16,3584]{2,1,0:T(8,128)(2,1)} %select_select_fusion), calls=%async_computation.1 | async-start | bytes 1835008 | tf_op jit(solution)/shard_map/all_to_all | solution.py:39
  89.8 26.8 %all-to-all-start.2 = ((bf16[8,16,3584]{2,1,0:T(8,128)(2,1)}), bf16[8,16,3584]{2,1,0:T(8,128)(2,1)S(1)}, u32[]{:S(2)}, u32[]{:S(2)}) async-start(bf16[8,16,3584]{2,1,0:T(8,128)(2,1)} %broadcast_select_fusion.1), calls=%async_computation.2 | async-start | bytes 1835008 | tf_op jit(solution)/shard_map/all_to_all | solution.py:64
  93.4 42.3 %all-reduce.2.cloned.1.call-start = ((), (), s32[]{:S(2)}) async-start(), calls=%async_computation.3 | async-start | bytes 1835008 | tf_op jit(solution)/shard_map/psum | solution.py:71
Sparse Core Ops, SparseCore 0:
  97.2 36.1 all-reduce.1
